TPU v7x, 32 devices: a whole 2x2x4 slice. The times are simulated.
32 devices in a mesh: row: 4 (over z), col: 8 (over y, x, core).
Axes of the slice: x: 2, y: 2, z: 4, core: 2. Of those that a mesh axis runs over, the one named last changes fastest.
Arguments:
- response_coeffs: float32 [3, 8192, 1024], P(None, ('row', 'col')), may hold values from -6 to 6
- occupied_coeffs: float32 [8192, 1024], P(('row', 'col')), may hold values from -0.1875 to 0.1875
Outputs:
- density: float32 [3, 8192, 8192], P(None, 'row', 'col')
All inputs are finite; a program needn't handle non-finite values.
Results may differ from a plain program's by a relative error of at most 0.0003.
Values sent between devices are 32-bit elements; how exact they have to be, the bound alone decides.
A program may use at most 256 MiB of HBM per device.

v0:
```python
import jax
import jax.numpy as jnp
from jax import lax
from jax.sharding import PartitionSpec as P

SLICE_PAIRS = ((0, 0), (0, 1), (1, 0))


def partner(value, axis, stride):
    mask = 2**stride
    pairs = [(source, source ^ mask) for source in range(lax.axis_size(axis))]
    return lax.ppermute(value, axis, pairs)


def split_slices(values):
    leading = lax.optimization_barrier(values.astype(jnp.bfloat16))
    remainder = values - leading.astype(jnp.float32)
    trailing = lax.optimization_barrier(remainder.astype(jnp.bfloat16))
    return [leading, trailing]


def contribute(row_slices, column_slices, perturbations):
    accumulated = jnp.zeros(
        (perturbations, row_slices[0].shape[1], column_slices[0].shape[1]), jnp.float32
    )
    for left_index, right_index in SLICE_PAIRS:
        forward_term = jnp.einsum(
            "kro,co->krc",
            row_slices[left_index][:perturbations],
            column_slices[right_index][perturbations],
            preferred_element_type=jnp.float32,
        )
        mirror_term = jnp.einsum(
            "ro,kco->krc",
            row_slices[right_index][perturbations],
            column_slices[left_index][:perturbations],
            preferred_element_type=jnp.float32,
        )
        accumulated = accumulated + forward_term + mirror_term
    return accumulated


def relay_columns(stacked, perturbations):
    rows_total = lax.axis_size("row")
    columns_total = lax.axis_size("col")
    col_index = lax.axis_index("col")
    shard_rows = stacked.shape[1]
    orbitals = stacked.shape[2]
    half_rows = shard_rows // 2
    swap_bit = rows_total.bit_length() - 1
    own_first = stacked[:, :half_rows]
    partner_second = partner(stacked[:, half_rows:], "col", swap_bit)
    even_first = col_index // rows_total == 0
    leading = jnp.where(even_first, own_first, partner_second)
    trailing = jnp.where(even_first, partner_second, own_first)
    paired = jnp.concatenate([leading, trailing], axis=1)
    gathered = lax.all_gather(paired, "row", axis=1, tiled=True)
    regrouped = lax.all_to_all(gathered, "col", split_axis=1, concat_axis=1, tiled=True)
    shaped = regrouped.reshape(perturbations + 1, 2, rows_total, half_rows, orbitals)
    flipped = shaped[:, ::-1]
    ordered = jnp.where(col_index % 2 == 0, shaped, flipped)
    return jnp.swapaxes(ordered, 1, 2).reshape(
        perturbations + 1, columns_total * half_rows, orbitals
    )


def shards(response_coeffs, occupied_coeffs):
    perturbations = response_coeffs.shape[0]
    stacked = jnp.concatenate([response_coeffs, occupied_coeffs[None]], axis=0)
    column_panel = relay_columns(stacked, perturbations)
    column_slices = split_slices(column_panel)
    return contribute(
        split_slices(lax.all_gather(stacked, "col", axis=1, tiled=True)),
        column_slices,
        perturbations,
    )


def solution(mesh):
    return jax.shard_map(
        shards,
        mesh=mesh,
        in_specs=(P(None, ("row", "col"), None), P(("row", "col"), None)),
        out_specs=P(None, "row", "col"),
        check_vma=False,
    )
```

profile of v0, /device:TPU:0, one launch (start us, length us, event | category | flops | bytes accessed | tf_op | source)
XLA Modules:
  0.0 913.4 jit_solution(8449333909172042322)
XLA Ops:
  6.5 0.0 copy-start.2
  6.5 0.0 all-gather.5.cloned.1.call-start
  6.5 3.2 fusion.7
  9.8 3.0 collective-permute-start
  12.8 45.9 %collective-permute-done = f32[4,128,1024]{2,1,0:T(8,128)} collective-permute-done((f32[4,128,1024]{2,1,0:T(8,128)}, f32[4,128,1024]{2,1,0:T(8,128)}, u32[]{:S(2)}, u32[]{:S(2)}) %collective-permute-start) | collective-permute-done | bytes 2097184 | tf_op jit(solution)/shard_map/ppermute | solution.py:12
  58.7 0.0 copy-done.2
  58.7 2.4 broadcast_select_fusion.1
  61.1 2.5 pad_maximum_fusion.1
  63.6 0.0 all-gather.5.cloned.1.call-update
  63.7 0.0 all-gather.3.cloned.1.call-start
  63.7 3.7 pad_maximum_fusion
  67.4 0.0 all-gather.3.cloned.1.call-update
  67.4 284.7 %all-gather.5.cloned.1.call-done = f32[4,1024,1024]{2,1,0:T(8,128)} async-done(((f32[4,256,1024]{2,1,0:T(8,128)}), f32[4,1024,1024]{2,1,0:T(8,128)}) %all-gather.5.cloned.1.call-update) | async-done | bytes 16777232 | tf_op jit(solution)/shard_map/all_gather | solution.py:57
  352.1 21.6 %copy.8 = f32[4,1024,1024]{2,0,1:T(4,128)} copy(f32[4,1024,1024]{2,1,0:T(8,128)} %all-gather.5.cloned.1.call-done) | data formatting | bytes 33554432 | tf_op jit(solution)/shard_map/all_gather | solution.py:57
  373.7 6.0 all-to-all-start
  379.7 302.3 %all-to-all-done = f32[4,1024,1024]{2,0,1:T(4,128)} async-done(((f32[4,1024,1024]{2,0,1:T(4,128)}), f32[4,1024,1024]{2,0,1:T(4,128)}, u32[]{:S(2)}, u32[]{:S(2)}) %all-to-all-start) | async-done | bytes 16777248 | tf_op jit(solution)/shard_map/all_to_all | solution.py:58
  682.0 15.2 %copy.10 = f32[4,2,4,128,1024]{4,3,1,2,0:T(8,128)S(1)} copy(f32[4,2,4,128,1024]{4,0,3,2,1:T(4,128)} %bitcast.1) | data formatting | bytes 33554432 | tf_op jit(solution)/shard_map/reshape | solution.py:59
  697.2 3.4 reverse_select_fusion
  700.6 2.4 bitcast_convert_fusion
  703.1 0.0 copy-start.1
  703.1 3.2 copy-done.1
  706.3 6.3 fusion.2
  712.6 0.0 all-gather.3.cloned.1.call-done
  712.6 12.1 %convert_element_type.18 = bf16[4,2048,1024]{2,1,0:T(8,128)(2,1)S(1)} convert(f32[4,2048,1024]{2,1,0:T(8,128)} %all-gather.3.cloned.1.call-done) | non-fusion elementwise | flops 8388608 | bytes 50331648 | tf_op jit(solution)/shard_map/convert_element_type | solution.py:16
  724.7 0.0 copy-start
  724.7 5.8 copy-done
  730.5 19.0 %fusion.4 = f32[3,1024,2048]{1,2,0:T(8,128)} fusion(bf16[4,1024,1024]{2,1,0:T(8,128)(2,1)} %fusion.2, bf16[4,2048,1024]{2,1,0:T(8,128)(2,1)S(1)} %convert_element_type.18), kind=kOutput, calls=%fused_computation.19 | convolution fusion | flops 12884901888 | bytes 37748736 | tf_op jit(solution)/shard_map/ro,kco->krc/dot_general | solution.py:33
  749.5 22.0 %fusion.8 = f32[3,2048,1024]{2,1,0:T(8,128)} fusion(bf16[4,2048,1024]{2,1,0:T(8,128)(2,1)} %copy-done, bf16[4,1024,1024]{2,1,0:T(8,128)(2,1)} %fusion.2), kind=kOutput, calls=%fused_computation.24 | convolution fusion | flops 12884901888 | bytes 44040192 | tf_op jit(solution)/shard_map/kro,co->krc/dot_general | solution.py:27
  771.5 0.0 slice-start
  771.5 0.0 slice-start.1
  771.5 21.8 %fusion.9 = f32[3,2048,1024]{2,1,0:T(8,128)} fusion(bf16[4,2048,1024]{2,1,0:T(8,128)(2,1)} %copy-done, bf16[4,1024,1024]{2,1,0:T(8,128)(2,1)} %copy-done.1), kind=kOutput, calls=%fused_computation.26 | convolution fusion | flops 12884901888 | bytes 44040192 | tf_op jit(solution)/shard_map/kro,co->krc/dot_general | solution.py:27
  793.3 0.0 slice-start.2
  793.3 0.0 slice-start.3
  793.3 20.0 %fusion.5 = f32[3,1024,2048]{1,2,0:T(8,128)} fusion(bf16[4,1024,1024]{2,1,0:T(8,128)(2,1)} %copy-done.1, bf16[4,2048,1024]{2,1,0:T(8,128)(2,1)} %copy-done), kind=kOutput, calls=%fused_computation.20 | convolution fusion | flops 12884901888 | bytes 37748736 | tf_op jit(solution)/shard_map/ro,kco->krc/dot_general | solution.py:33
  813.3 0.0 slice-done
  813.3 0.0 slice-done.1
  813.3 0.0 slice-done.2
  813.3 0.0 slice-done.3
  813.3 19.5 %subtract_convert_fusion = bf16[4,2048,1024]{2,1,0:T(8,128)(2,1)} fusion(f32[4,2048,1024]{2,1,0:T(8,128)} %all-gather.3.cloned.1.call-done, bf16[4,2048,1024]{2,1,0:T(8,128)(2,1)S(1)} %bitcast.54), kind=kLoop, calls=%fused_computation | loop fusion | flops 25165824 | bytes 67108864 | tf_op jit(solution)/shard_map/convert_element_type | solution.py:18
  832.8 20.0 %fusion.3 = f32[3,1024,2048]{1,2,0:T(8,128)} fusion(bf16[4,1024,1024]{2,1,0:T(8,128)(2,1)} %copy-done.1, bf16[4,2048,1024]{2,1,0:T(8,128)(2,1)} %subtract_convert_fusion), kind=kOutput, calls=%fused_computation.16 | convolution fusion | flops 12884901888 | bytes 37748736 | tf_op jit(solution)/shard_map/ro,kco->krc/dot_general | solution.py:33
  852.8 53.5 %bitcast_add_fusion = f32[3,2048,1024]{2,1,0:T(8,128)} fusion(f32[3,1024,2048]{1,2,0:T(8,128)} %fusion.4, f32[3,1024,2048]{1,2,0:T(8,128)} %fusion.3, f32[3,2048,1024]{2,1,0:T(8,128)} %fusion.8, f32[3,2048,1024]{2,1,0:T(8,128)} %fusion.9, f32[3,1024,2048]{1,2,0:T(8,128)} %fusion.5, bf16[4,2048,1024]{2,1,0:T(8,128)(2,1)} %subtract_convert_fusion, ...), kind=kOutput, calls=%fused_computation.1 | convolution fusion | flops 12916359168 | bytes 169869312 | tf_op jit(solution)/shard_map/kro,co->krc/dot_general | solution.py:27
  (1 shorter events, 0.0 us)
Async XLA Ops:
  6.5 52.2 %copy-start.2 = (f32[3,256,1024]{2,1,0:T(8,128)S(1)}, f32[3,256,1024]{2,1,0:T(8,128)}, u32[]{:S(2)}) copy-start(f32[3,256,1024]{2,1,0:T(8,128)} %param.2) | copy-start | bytes 9437188
  6.5 345.5 %all-gather.5.cloned.1.call-start = ((), (), s32[]{:S(2)}) async-start(), calls=%async_computation.2 | async-start | bytes 20971520 | tf_op jit(solution)/shard_map/all_gather | solution.py:57
  9.8 48.9 %collective-permute-start = (f32[4,128,1024]{2,1,0:T(8,128)}, f32[4,128,1024]{2,1,0:T(8,128)}, u32[]{:S(2)}, u32[]{:S(2)}) collective-permute-start(f32[4,128,1024]{2,1,0:T(8,128)} %fusion.7), channel_id=1, source_target_pairs={{0,4},{1,5},{2,6},{3,7},{4,0},{5,1},{6,2},{7,3},{8,12},{9,13},{10,... | collective-permute-start | bytes 6291464 | tf_op jit(solution)/shard_map/ppermute | solution.py:12
  63.7 648.9 %all-gather.3.cloned.1.call-start = ((), (), s32[]{:S(2)}) async-start(), calls=%async_computation.1 | async-start | bytes 37748736 | tf_op jit(solution)/shard_map/all_gather | solution.py:73
  373.7 308.3 %all-to-all-start = ((f32[4,1024,1024]{2,0,1:T(4,128)}), f32[4,1024,1024]{2,0,1:T(4,128)}, u32[]{:S(2)}, u32[]{:S(2)}) async-start(f32[4,1024,1024]{2,0,1:T(4,128)} %copy.8), calls=%async_computation | async-start | bytes 33554432 | tf_op jit(solution)/shard_map/all_to_all | solution.py:58
  703.1 3.2 copy-start.1
  724.7 5.8 copy-start
  771.5 41.8 %slice-start = ((s8[16777216]{0:T(1024)(128)(4,1)}), s8[4194304]{0:T(1024)(128)(4,1)S(1)}, s32[]{:S(2)}) async-start(s8[16777216]{0:T(1024)(128)(4,1)} %bitcast.53), calls=%async_computation.3 | async-start | bytes 8388608
  771.5 41.8 %slice-start.1 = ((s8[16777216]{0:T(1024)(128)(4,1)}), s8[4194304]{0:T(1024)(128)(4,1)S(1)}, s32[]{:S(2)}) async-start(s8[16777216]{0:T(1024)(128)(4,1)} %bitcast.53), calls=%async_computation.4 | async-start | bytes 8388608
  793.3 20.0 %slice-start.2 = ((s8[16777216]{0:T(1024)(128)(4,1)}), s8[4194304]{0:T(1024)(128)(4,1)S(1)}, s32[]{:S(2)}) async-start(s8[16777216]{0:T(1024)(128)(4,1)} %bitcast.53), calls=%async_computation.5 | async-start | bytes 8388608
  793.3 20.0 %slice-start.3 = ((s8[16777216]{0:T(1024)(128)(4,1)}), s8[4194304]{0:T(1024)(128)(4,1)S(1)}, s32[]{:S(2)}) async-start(s8[16777216]{0:T(1024)(128)(4,1)} %bitcast.53), calls=%async_computation.6 | async-start | bytes 8388608
Sparse Core Ops, SparseCore 0:
  63.8 288.2 all-gather.4
  353.9 325.4 all-gather.2
where the time goes:
time: 918 us; the launch traced here: 913 us
  waiting for transfers between devices  633 us (69%)
  matrix products  156 us (17%)
  other arithmetic  55.5 us (6%)
  local copies, waits for them, and re-layouts  45.9 us (5%)
  between operations  13.7 us (1%)
    all_to_all x1, waiting for transfers between devices, relay_columns(): lax.all_to_all(gathered, 'col', split_axis=1, concat_axis=1, tiled=True)  302 us
    all_gather x1, waiting for transfers between devices, relay_columns(): gathered = lax.all_gather(paired, 'row', axis=1, tiled=True)  285 us
    dot_general x3, matrix products, contribute(): jnp.einsum('kro,co->krc', row_slices[left_index][:perturbations], column_...  97.3 us
    dot_general x3, matrix products, contribute(): jnp.einsum('ro,kco->krc', row_slices[right_index][perturbations], column_...  59 us
    ppermute x1, waiting for transfers between devices, partner(): return lax.ppermute(value, axis, pairs)  45.9 us
    convert_element_type x2, other arithmetic, split_slices(): trailing = lax.optimization_barrier(remainder.astype(jnp.bfloat16))  25.8 us
    all_gather x1, local copies, waits for them, and re-layouts, relay_columns(): gathered = lax.all_gather(paired, 'row', axis=1, tiled=True)  21.6 us
  transfers between devices with their start and end apart: 4, of which 3 were waited for; matrix products, arithmetic and copies ran while one was open for 6% of the time, Pallas kernels for 0%

commit v1 on v0

--- a/solution.py
+++ b/solution.py
@@ -54,7 +54,12 @@
     leading = jnp.where(even_first, own_first, partner_second)
     trailing = jnp.where(even_first, partner_second, own_first)
     paired = jnp.concatenate([leading, trailing], axis=1)
-    gathered = lax.all_gather(paired, "row", axis=1, tiled=True)
+    ring = [paired]
+    for hop in range(3):
+        ring.append(lax.ppermute(ring[-1], "row", [(dev, (dev + 1) % 4) for dev in range(4)]))
+    gathered = jnp.roll(
+        jnp.concatenate(ring[::-1], axis=1), (lax.axis_index("row") + 1) * ring[0].shape[1], axis=1
+    )
     regrouped = lax.all_to_all(gathered, "col", split_axis=1, concat_axis=1, tiled=True)
     shaped = regrouped.reshape(perturbations + 1, 2, rows_total, half_rows, orbitals)
     flipped = shaped[:, ::-1]

time: 918 us -> 861 us (0.938)
  waiting for transfers between devices: 633 us -> 534 us
  local copies, waits for them, and re-layouts: 45.9 us -> 91.7 us
    all_gather x1 -> x0, waiting for transfers between devices: 285 us -> none  [relay_columns(): gathered = lax.all_gather(paired, 'row', axis=1, tiled=True)]
    ppermute x0 -> x3, waiting for transfers between devices: none -> 270 us  [relay_columns(): lax.ppermute(ring[-1], 'row', [(dev, (dev + 1) % 4) for dev in range(4)])]
    all_to_all x1, waiting for transfers between devices: 302 us -> 184 us  [relay_columns(): lax.all_to_all(gathered, 'col', split_axis=1, concat_axis=1, tiled=True)]
    unnamed x14 -> x29, local copies, waits for them, and re-layouts: 9.03 us -> 46.7 us
    ppermute x1, waiting for transfers between devices: 45.9 us -> 80.3 us  [partner(): return lax.ppermute(value, axis, pairs)]
    dynamic_slice x0 -> x2, local copies, waits for them, and re-layouts: none -> 28.4 us  [relay_columns(): jnp.roll(jnp.concatenate(ring[::-1], axis=1), (lax.axis_index('row') + 1)...]
    all_gather x1 -> x0, local copies, waits for them, and re-layouts: 21.6 us -> none  [relay_columns(): gathered = lax.all_gather(paired, 'row', axis=1, tiled=True)]
  transfers between devices with their start and end apart: 4 -> 6, of which waited for: 3 -> 5; matrix products, arithmetic and copies ran while one was open for 6% -> 11% of each run, Pallas kernels for 0% -> 0%
where the time goes in v1:
time: 861 us; the launch traced here: 855 us
  waiting for transfers between devices  534 us (62%)
  matrix products  153 us (18%)
  local copies, waits for them, and re-layouts  91.7 us (11%)
  other arithmetic  51.4 us (6%)
  between operations  13.8 us (2%)
  starting transfers between devices  10.8 us (1%)
    ppermute x3, waiting for transfers between devices, relay_columns(): lax.ppermute(ring[-1], 'row', [(dev, (dev + 1) % 4) for dev in range(4)])  270 us
    all_to_all x1, waiting for transfers between devices, relay_columns(): lax.all_to_all(gathered, 'col', split_axis=1, concat_axis=1, tiled=True)  184 us
    dot_general x3, matrix products, contribute(): jnp.einsum('kro,co->krc', row_slices[left_index][:perturbations], column_...  96.5 us
    ppermute x1, waiting for transfers between devices, partner(): return lax.ppermute(value, axis, pairs)  80.3 us
    dot_general x3, matrix products, contribute(): jnp.einsum('ro,kco->krc', row_slices[right_index][perturbations], column_...  56.5 us
    unnamed x29, local copies, waits for them, and re-layouts  46.7 us
    dynamic_slice x2, local copies, waits for them, and re-layouts, relay_columns(): jnp.roll(jnp.concatenate(ring[::-1], axis=1), (lax.axis_index('row') + 1)...  28.4 us
    convert_element_type x2, other arithmetic, split_slices(): trailing = lax.optimization_barrier(remainder.astype(jnp.bfloat16))  23.2 us
  transfers between devices with their start and end apart: 6, of which 5 were waited for; matrix products, arithmetic and copies ran while one was open for 11% of the time, Pallas kernels for 0%

profile of v1, /device:TPU:0, one launch (start us, length us, event | category | flops | bytes accessed | tf_op | source)
XLA Modules:
  0.0 854.9 jit_solution(3209215302972781116)
XLA Ops:
  6.5 0.0 all-gather.2.cloned.1.call-start
  6.5 4.9 pad_maximum_fusion
  11.4 0.0 all-gather.2.cloned.1.call-update
  11.4 1.7 fusion.7
  13.1 3.1 collective-permute-start
  16.2 80.3 %collective-permute-done = f32[4,128,1024]{2,1,0:T(8,128)} collective-permute-done((f32[4,128,1024]{2,1,0:T(8,128)S(1)}, f32[4,128,1024]{2,1,0:T(8,128)}, u32[]{:S(2)}, u32[]{:S(2)}) %collective-permute-start) | collective-permute-done | bytes 2097184 | tf_op jit(solution)/shard_map/ppermute | solution.py:12
  96.4 0.0 copy-done.7
  96.5 3.1 broadcast_select_fusion.1
  99.6 1.4 copy-done.3
  101.0 0.6 pad_maximum_fusion.1
  101.6 1.6 collective-permute-start.1
  103.1 89.7 %collective-permute-done.1 = f32[4,256,1024]{2,1,0:T(8,128)S(1)} collective-permute-done((f32[4,256,1024]{2,1,0:T(8,128)S(1)}, f32[4,256,1024]{2,1,0:T(8,128)S(1)}, u32[]{:S(2)}, u32[]{:S(2)}) %collective-permute-start.1) | collective-permute-done | bytes 4194336 | tf_op jit(solution)/shard_map/ppermute | solution.py:59
  192.8 2.0 copy-done.5
  194.8 0.0 collective-permute-start.2
  194.8 90.5 %collective-permute-done.2 = f32[4,256,1024]{2,1,0:T(8,128)} collective-permute-done((f32[4,256,1024]{2,1,0:T(8,128)S(1)}, f32[4,256,1024]{2,1,0:T(8,128)}, u32[]{:S(2)}, u32[]{:S(2)}) %collective-permute-start.2) | collective-permute-done | bytes 4194336 | tf_op jit(solution)/shard_map/ppermute | solution.py:59
  285.3 0.0 collective-permute-start.3
  285.3 89.8 %collective-permute-done.3 = f32[4,256,1024]{2,1,0:T(8,128)} collective-permute-done((f32[4,256,1024]{2,1,0:T(8,128)}, f32[4,256,1024]{2,1,0:T(8,128)}, u32[]{:S(2)}, u32[]{:S(2)}) %collective-permute-start.3) | collective-permute-done | bytes 4194336 | tf_op jit(solution)/shard_map/ppermute | solution.py:59
  375.1 4.8 constant_dynamic-update-slice_fusion.9
  379.9 4.9 constant_dynamic-update-slice_fusion.8
  384.7 2.3 constant_dynamic-update-slice_fusion.7
  387.0 0.0 copy-done.4
  387.0 1.6 constant_dynamic-update-slice_fusion.6
  388.6 1.5 constant_dynamic-update-slice_fusion.5
  390.0 4.8 constant_dynamic-update-slice_fusion.4
  394.8 4.8 constant_dynamic-update-slice_fusion.3
  399.6 2.3 constant_dynamic-update-slice_fusion.2
  402.0 1.5 constant_dynamic-update-slice_fusion.1
  403.5 1.5 constant_dynamic-update-slice_fusion
  405.0 6.6 constant_dynamic-slice_fusion
  411.5 21.9 %copy.8 = f32[4,1024,1024]{2,0,1:T(4,128)} copy(f32[4,1024,1024]{2,1,0:T(8,128)S(1)} %constant_dynamic-slice_fusion) | data formatting | bytes 33554432 | tf_op jit(solution)/shard_map/jit(_roll_dynamic)/dynamic_slice | solution.py:60
  433.4 6.2 all-to-all-start
  439.6 183.9 %all-to-all-done = f32[4,1024,1024]{2,0,1:T(4,128)} async-done(((f32[4,1024,1024]{2,0,1:T(4,128)}), f32[4,1024,1024]{2,0,1:T(4,128)}, u32[]{:S(2)}, u32[]{:S(2)}) %all-to-all-start) | async-done | bytes 16777248 | tf_op jit(solution)/shard_map/all_to_all | solution.py:63
  623.5 15.2 %copy.10 = f32[4,2,4,128,1024]{4,3,1,2,0:T(8,128)S(1)} copy(f32[4,2,4,128,1024]{4,0,3,2,1:T(4,128)} %bitcast.1) | data formatting | bytes 33554432 | tf_op jit(solution)/shard_map/reshape | solution.py:64
  638.7 3.4 reverse_select_fusion
  642.1 2.4 bitcast_convert_fusion
  644.6 3.2 copy-done.2
  647.8 6.3 fusion.2
  654.1 12.1 %convert_element_type.18 = bf16[4,2048,1024]{2,1,0:T(8,128)(2,1)S(1)} convert(f32[4,2048,1024]{2,1,0:T(8,128)} %all-gather.2.cloned.1.call-done) | non-fusion elementwise | flops 8388608 | bytes 50331648 | tf_op jit(solution)/shard_map/convert_element_type | solution.py:16
  666.2 5.8 copy-done
  672.0 19.1 %fusion.4 = f32[3,1024,2048]{1,2,0:T(8,128)} fusion(bf16[4,1024,1024]{2,1,0:T(8,128)(2,1)} %fusion.2, bf16[4,2048,1024]{2,1,0:T(8,128)(2,1)S(1)} %convert_element_type.18), kind=kOutput, calls=%fused_computation.19 | convolution fusion | flops 12884901888 | bytes 37748736 | tf_op jit(solution)/shard_map/ro,kco->krc/dot_general | solution.py:33
  691.2 21.8 %fusion.8 = f32[3,2048,1024]{2,1,0:T(8,128)} fusion(bf16[4,2048,1024]{2,1,0:T(8,128)(2,1)} %copy-done, bf16[4,1024,1024]{2,1,0:T(8,128)(2,1)} %fusion.2), kind=kOutput, calls=%fused_computation.24 | convolution fusion | flops 12884901888 | bytes 44040192 | tf_op jit(solution)/shard_map/kro,co->krc/dot_general | solution.py:27
  713.0 0.0 slice-done.1
  713.0 18.6 %fusion.5 = f32[3,1024,2048]{1,2,0:T(8,128)} fusion(bf16[4,1024,1024]{2,1,0:T(8,128)(2,1)S(1)} %bitcast.54, bf16[4,2048,1024]{2,1,0:T(8,128)(2,1)} %copy-done), kind=kOutput, calls=%fused_computation.20 | convolution fusion | flops 12884901888 | bytes 37748736 | tf_op jit(solution)/shard_map/ro,kco->krc/dot_general | solution.py:33
  731.5 21.2 %fusion.9 = f32[3,2048,1024]{2,1,0:T(8,128)} fusion(bf16[4,2048,1024]{2,1,0:T(8,128)(2,1)} %copy-done, bf16[4,1024,1024]{2,1,0:T(8,128)(2,1)S(1)} %bitcast.54), kind=kOutput, calls=%fused_computation.26 | convolution fusion | flops 12884901888 | bytes 44040192 | tf_op jit(solution)/shard_map/kro,co->krc/dot_general | solution.py:27
  752.7 16.9 %subtract_convert_fusion = bf16[4,2048,1024]{2,1,0:T(8,128)(2,1)S(1)} fusion(f32[4,2048,1024]{2,1,0:T(8,128)} %all-gather.2.cloned.1.call-done, bf16[4,2048,1024]{2,1,0:T(8,128)(2,1)} %copy-done), kind=kLoop, calls=%fused_computation | loop fusion | flops 25165824 | bytes 67108864 | tf_op jit(solution)/shard_map/convert_element_type | solution.py:18
  769.6 5.8 copy-done.1
  775.5 18.8 %fusion.3 = f32[3,1024,2048]{1,2,0:T(8,128)} fusion(bf16[4,1024,1024]{2,1,0:T(8,128)(2,1)} %copy-done.2, bf16[4,2048,1024]{2,1,0:T(8,128)(2,1)S(1)} %subtract_convert_fusion), kind=kOutput, calls=%fused_computation.16 | convolution fusion | flops 12884901888 | bytes 37748736 | tf_op jit(solution)/shard_map/ro,kco->krc/dot_general | solution.py:33
  794.3 53.5 %bitcast_add_fusion = f32[3,2048,1024]{2,1,0:T(8,128)} fusion(f32[3,1024,2048]{1,2,0:T(8,128)} %fusion.4, f32[3,1024,2048]{1,2,0:T(8,128)} %fusion.3, f32[3,2048,1024]{2,1,0:T(8,128)} %fusion.8, f32[3,2048,1024]{2,1,0:T(8,128)} %fusion.9, f32[3,1024,2048]{1,2,0:T(8,128)} %fusion.5, bf16[4,2048,1024]{2,1,0:T(8,128)(2,1)} %copy-done.1, ...), kind=kOutput, calls=%fused_computation.1 | convolution fusion | flops 12916359168 | bytes 169869312 | tf_op jit(solution)/shard_map/kro,co->krc/dot_general | solution.py:27
  (14 shorter events, 0.0 us)
Async XLA Ops:
  6.5 89.9 %copy-start.7 = (f32[256,1024]{1,0:T(8,128)S(1)}, f32[256,1024]{1,0:T(8,128)}, u32[]{:S(2)}) copy-start(f32[256,1024]{1,0:T(8,128)} %param.3) | copy-start | bytes 3145732
  6.5 647.5 %all-gather.2.cloned.1.call-start = ((), (), s32[]{:S(2)}) async-start(), calls=%async_computation.1 | async-start | bytes 37748736 | tf_op jit(solution)/shard_map/all_gather | solution.py:78
  13.1 83.4 %collective-permute-start = (f32[4,128,1024]{2,1,0:T(8,128)S(1)}, f32[4,128,1024]{2,1,0:T(8,128)}, u32[]{:S(2)}, u32[]{:S(2)}) collective-permute-start(f32[4,128,1024]{2,1,0:T(8,128)S(1)} %fusion.7), channel_id=1, source_target_pairs={{0,4},{1,5},{2,6},{3,7},{4,0},{5,1},{6,2},{7,3},{8,12},{9,13},{10,... | collective-permute-start | bytes 6291464 | tf_op jit(solution)/shard_map/ppermute | solution.py:12
  99.6 1.4 copy-start.3
  101.6 91.2 %collective-permute-start.1 = (f32[4,256,1024]{2,1,0:T(8,128)S(1)}, f32[4,256,1024]{2,1,0:T(8,128)S(1)}, u32[]{:S(2)}, u32[]{:S(2)}) collective-permute-start(f32[4,256,1024]{2,1,0:T(8,128)S(1)} %pad_maximum_fusion.1), channel_id=1, source_target_pairs={{0,8},{8,16},{16,24},{24,0},{1,9},{9,17},{17,25},{25,1},{2,10},{10... | collective-permute-start | bytes 12582920 | tf_op jit(solution)/shard_map/ppermute | solution.py:59
  192.8 2.0 copy-start.5
  194.8 90.5 %collective-permute-start.2 = (f32[4,256,1024]{2,1,0:T(8,128)S(1)}, f32[4,256,1024]{2,1,0:T(8,128)}, u32[]{:S(2)}, u32[]{:S(2)}) collective-permute-start(f32[4,256,1024]{2,1,0:T(8,128)S(1)} %collective-permute-done.1), channel_id=1, source_target_pairs={{0,8},{8,16},{16,24},{24,0},{1,9},{9,17},{17,25},{25,1},{2,10},{10... | collective-permute-start | bytes 12582920 | tf_op jit(solution)/shard_map/ppermute | solution.py:59
  285.3 89.8 %collective-permute-start.3 = (f32[4,256,1024]{2,1,0:T(8,128)}, f32[4,256,1024]{2,1,0:T(8,128)}, u32[]{:S(2)}, u32[]{:S(2)}) collective-permute-start(f32[4,256,1024]{2,1,0:T(8,128)} %collective-permute-done.2), channel_id=1, source_target_pairs={{0,8},{8,16},{16,24},{24,0},{1,9},{9,17},{17,25},{25,1},{2,10},{10... | collective-permute-start | bytes 12582920 | tf_op jit(solution)/shard_map/ppermute | solution.py:59
  285.3 99.4 %copy-start.6 = (f32[4,256,1024]{2,1,0:T(8,128)S(1)}, f32[4,256,1024]{2,1,0:T(8,128)}, u32[]{:S(2)}) copy-start(f32[4,256,1024]{2,1,0:T(8,128)} %copy-done.5) | copy-start | bytes 12582916
  285.3 101.7 %copy-start.4 = (f32[4,128,1024]{2,1,0:T(8,128)S(1)}, f32[4,128,1024]{2,1,0:T(8,128)}, u32[]{:S(2)}) copy-start(f32[4,128,1024]{2,1,0:T(8,128)} %copy-done.3) | copy-start | bytes 6291460
  433.4 190.1 %all-to-all-start = ((f32[4,1024,1024]{2,0,1:T(4,128)}), f32[4,1024,1024]{2,0,1:T(4,128)}, u32[]{:S(2)}, u32[]{:S(2)}) async-start(f32[4,1024,1024]{2,0,1:T(4,128)} %copy.8), calls=%async_computation | async-start | bytes 33554432 | tf_op jit(solution)/shard_map/all_to_all | solution.py:63
  644.6 3.2 copy-start.2
  666.2 5.8 copy-start
  672.0 40.9 %slice-start = ((s8[8388608]{0:T(1024)(128)(4,1)}), s8[4194304]{0:T(1024)(128)(4,1)S(1)}, s32[]{:S(2)}) async-start(s8[8388608]{0:T(1024)(128)(4,1)} %bitcast.53), calls=%async_computation.2 | async-start | bytes 8388608
  691.1 21.8 %slice-start.1 = ((s8[8388608]{0:T(1024)(128)(4,1)}), s8[4194304]{0:T(1024)(128)(4,1)S(1)}, s32[]{:S(2)}) async-start(s8[8388608]{0:T(1024)(128)(4,1)} %bitcast.53), calls=%async_computation.3 | async-start | bytes 8388608
  769.6 5.8 copy-start.1
Sparse Core Ops, SparseCore 0:
  11.6 197.7 all-gather.1
